TPU v7x, 256 devices: a whole 4x4x8 slice. The times are simulated.
256 devices in a mesh: dp: 8 (over x, core), tensor: 16 (over y, z_lo), pipe: 2 (over z_hi).
Axes of the slice: x: 4, y: 4, z: 8 (z_hi: 2, z_lo: 4; z = z_hi * 4 + z_lo), core: 2. Of those that a mesh axis runs over, the one named last changes fastest.
Arguments:
- hidden: bfloat16 [2, 1024, 7168], P('pipe', ('dp', 'tensor')), may hold values from -200 to 200
- head_table: bfloat16 [81920, 7168], P(('dp', 'tensor')), may hold values from -1 to 1
- targets: int32 [2, 1024], P('pipe', ('dp', 'tensor')), may hold values from 0 to 81919
Outputs:
- token_loss: float32 [2, 1024], P('pipe', ('dp', 'tensor'))
- mean_loss: float32 [], replicated
All inputs are finite; a program needn't handle non-finite values.
Results may differ from a plain program's by a relative error of at most 0.0003.
Values may be sent and summed in bfloat16 or wider, within the bound.
A program may use at most 128 MiB of HBM per device.

v0:
```python
import jax
import jax.numpy as jnp
from jax import lax
from jax.sharding import Mesh
from jax.sharding import PartitionSpec as P

DP_TENSOR = ("dp_0", "dp_1", "tensor_0", "tensor_1")


def in_order(pieces, dim):
    lengths = list(pieces.shape[1:])
    lengths[dim] *= pieces.shape[0]
    return jnp.moveaxis(pieces, 0, dim).reshape(lengths)


def gather_in_order(value, axes, order):
    pieces = value
    for k in order:
        pieces = lax.all_gather(pieces, axes[k])
    done = order[::-1]
    back = [done.index(k) for k in range(len(axes))]
    pieces = pieces.transpose(*back, *range(len(axes), pieces.ndim))
    return pieces.reshape(-1, *value.shape)


def gather_axes(value, axes, order, dim):
    return in_order(gather_in_order(value, axes, order), dim)


def all_in_one(value, axis):
    leaves = jax.tree.leaves(value)
    order = sorted(range(len(leaves)), key=lambda k: -leaves[k].size)
    width = (1, *leaves[order[0]].shape)[-1]
    lines = [
        jnp.pad(leaves[k].reshape(-1), (0, -leaves[k].size % width)).reshape(-1, width)
        for k in order
    ]
    both, at, found = (lax.all_gather(jnp.concatenate(lines), axis), 0, {})
    for k, line in zip(order, lines):
        piece = both[:, at : at + len(line)].reshape(len(both), -1)
        found[k] = piece[:, : leaves[k].size].reshape(-1, *leaves[k].shape)
        at += len(line)
    numbers = iter(range(len(leaves)))
    return jax.tree.map(lambda _: found[next(numbers)], value)


def combined_by_axis(value, axes, combine):
    for axis in axes:
        pieces = all_in_one(value, axis)
        value = jax.tree.map(lambda part: part[0], pieces)
        for k in range(1, lax.axis_size(axis)):
            value = combine(value, jax.tree.map(lambda part: part[k], pieces))
    return value


def copy_for_each(value, axis):
    devices = lax.axis_size(axis)
    return lax.all_to_all(
        jnp.broadcast_to(value[None], (devices, *value.shape)), axis, 0, 0, tiled=True
    )


def of_everyone(value, axis):
    everything = copy_for_each(value, axis)
    return jnp.sum(everything, axis=0)


def combine_stats(earlier, later):
    maxima = jnp.maximum(earlier[0], later[0])
    totals = earlier[1] * jnp.exp(earlier[0] - maxima) + later[1] * jnp.exp(later[0] - maxima)
    return (maxima, totals, earlier[2] + later[2])


def body(hidden, head_table, targets):
    row_count = head_table.shape[0]
    position = lax.axis_index(DP_TENSOR)
    offset = position * row_count
    tokens_own = hidden[0]
    labels_own = targets[0]
    own_count = tokens_own.shape[0]
    columns = lax.broadcasted_iota(jnp.int32, (1, row_count), 1)
    gathered, labels = (
        gather_axes(tokens_own, DP_TENSOR, (3, 0, 2, 1), 0),
        gather_axes(labels_own, DP_TENSOR, (3, 0, 2, 1), 0),
    )
    logits = lax.dot_general(
        gathered, head_table, (((1,), (1,)), ((), ())), preferred_element_type=jnp.float32
    )
    local_ids = (labels - offset)[:, None]
    picked = jnp.sum(jnp.where(columns == local_ids, logits, 0.0), axis=1)
    logits, picked = (logits, picked)
    local_maxima = jnp.max(logits, axis=1)
    exp_sums = jnp.sum(jnp.exp(logits - local_maxima[:, None]), axis=1)
    maxima, totals, chosen = combined_by_axis(
        (local_maxima, exp_sums, picked), DP_TENSOR, combine_stats
    )
    losses = maxima + jnp.log(totals) - chosen
    own_losses = lax.dynamic_slice_in_dim(losses, position * own_count, own_count, 0)
    loss_sum = of_everyone(jnp.sum(losses), "pipe")
    mean_loss = loss_sum / (losses.shape[0] * lax.axis_size("pipe"))
    return (own_losses[None, :], mean_loss)


def solution(mesh):
    split = Mesh(
        mesh.devices.reshape(4, 2, 4, 4, mesh.shape["pipe"]),
        ("dp_0", "dp_1", "tensor_0", "tensor_1", "pipe"),
    )
    return jax.shard_map(
        body,
        mesh=split,
        in_specs=(P("pipe", DP_TENSOR, None), P(DP_TENSOR, None), P("pipe", DP_TENSOR)),
        out_specs=(P("pipe", DP_TENSOR), P()),
        check_vma=False,
    )
```

profile of v0, /device:TPU:2, one launch (start us, length us, event | category | flops | bytes accessed | tf_op | source)
XLA Modules:
  0.0 256.2 jit_solution(10956692664639280291)
XLA Ops:
  7.2 0.0 all-gather.20.cloned.1.call-start
  7.2 18.1 %all_gather.66 = bf16[4,8,7168]{2,1,0:T(8,128)(2,1)} all-gather(bf16[1,8,7168]{2,1,0:T(8,128)(2,1)} %param.3), channel_id=1, replica_groups=mesh['dp_0'=4,'dp_1'=2,'tensor_0'=4,'tensor_1'=4,'pipe'=2] {'tensor_1'}, dimensions={0}, use_global_device_ids=true | all-gather | bytes 573440 | tf_op jit(solution)/shard_map/all_gather | solution.py:19
  25.3 0.0 all-gather.20.cloned.1.call-update
  25.3 0.0 all-gather.22.cloned.1.call-start
  25.4 30.6 %all-gather.20.cloned.1.call-done = bf16[16,8,7168]{2,1,0:T(8,128)(2,1)} async-done(((bf16[4,8,7168]{2,1,0:T(8,128)(2,1)}), bf16[16,8,7168]{2,1,0:T(8,128)(2,1)}) %all-gather.20.cloned.1.call-update) | async-done | bytes 1835024 | tf_op jit(solution)/shard_map/all_gather | solution.py:19
  56.0 0.0 all-gather.22.cloned.1.call-update
  56.0 0.0 all-gather.24.cloned.1.call-start
  56.1 79.7 %all-gather.22.cloned.1.call-done = bf16[16,4,8,7168]{3,2,1,0:T(8,128)(2,1)} async-done(((bf16[4,4,8,7168]{3,2,1,0:T(8,128)(2,1)}), bf16[16,4,8,7168]{3,2,1,0:T(8,128)(2,1)}) %all-gather.22.cloned.1.call-update) | async-done | bytes 7340048 | tf_op jit(solution)/shard_map/all_gather | solution.py:19
  135.8 0.0 copy-start
  135.8 0.0 all-gather.24.cloned.1.call-update
  135.8 0.6 copy-done
  136.4 11.1 %all-gather.10 = s32[4,1,8]{2,1,0:T(1,128)S(1)} all-gather(s32[1,1,8]{2,1,0:T(1,128)S(1)} %bitcast.236), channel_id=1, replica_groups=mesh['dp_0'=4,'dp_1'=2,'tensor_0'=4,'tensor_1'=4,'pipe'=2] {'tensor_1'}, dimensions={0}, use_global_device_ids=true | all-gather | bytes 160 | tf_op jit(solution)/shard_map/all_gather | solution.py:19
  147.5 10.8 %all-gather.11 = s32[4,4,8]{2,1,0:T(4,128)S(1)} all-gather(s32[1,4,8]{2,1,0:T(4,128)S(1)} %bitcast.235), channel_id=5, replica_groups=mesh['dp_0'=4,'dp_1'=2,'tensor_0'=4,'tensor_1'=4,'pipe'=2] {'dp_0'}, dimensions={0}, use_global_device_ids=true | all-gather | bytes 640 | tf_op jit(solution)/shard_map/all_gather | solution.py:19
  158.3 11.9 %all-gather.4 = s32[16,4,8]{2,1,0:T(4,128)S(1)} all-gather(s32[4,4,8]{2,1,0:T(4,128)S(1)} %all-gather.11), channel_id=6, replica_groups=mesh['dp_0'=4,'dp_1'=2,'tensor_0'=4,'tensor_1'=4,'pipe'=2] {'tensor_0'}, dimensions={0}, use_global_device_ids=true | all-gather | bytes 2560 | tf_op jit(solution)/shard_map/all_gather | solution.py:19
  170.2 1.8 all-gather.5
  172.1 0.1 sub.190
  172.2 0.0 all-gather.24.cloned.1.call-done
  172.2 7.4 %copy.12 = bf16[8,4,4,8,7168]{4,3,2,0,1:T(8,128)(2,1)S(1)} copy(bf16[8,4,4,8,7168]{4,3,2,1,0:T(8,128)(2,1)} %all-gather.24.cloned.1.call-done) | data formatting | bytes 29360128 | tf_op jit(solution)/shard_map/all_gather | solution.py:19
  179.7 12.3 %fusion.42 = (f32[1024]{0:T(1024)S(1)}, f32[1024,640]{0,1:T(8,128)S(1)}) fusion(bf16[1024,7168]{1,0:T(8,128)(2,1)S(1)} %bitcast.216, bf16[640,7168]{1,0:T(8,128)(2,1)} %param.4), kind=kOutput, calls=%fused_computation.83 | convolution fusion | flops 9395895296 | bytes 26480640 | tf_op jit(solution)/shard_map/dot_general | solution.py:86
  192.0 0.7 exponential_reduce_fusion
  192.7 11.3 %all-gather.12 = f32[4,3,1024]{2,1,0:T(4,128)S(1)} all-gather(f32[1,3,1024]{2,1,0:T(4,128)S(1)} %maximum_bitcast_fusion), channel_id=8, replica_groups=mesh['dp_0'=4,'dp_1'=2,'tensor_0'=4,'tensor_1'=4,'pipe'=2] {'dp_0'}, dimensions={0}, use_global_device_ids=true | all-gather | bytes 61440 | tf_op jit(solution)/shard_map/all_gather | solution.py:38
  204.0 0.1 fusion.16
  204.1 1.8 all-gather.13
  206.0 11.9 %all-gather.14 = f32[4,3,1024]{2,1,0:T(4,128)S(1)} all-gather(f32[1,3,1024]{2,1,0:T(4,128)S(1)} %maximum_bitcast_fusion.2), channel_id=10, replica_groups=mesh['dp_0'=4,'dp_1'=2,'tensor_0'=4,'tensor_1'=4,'pipe'=2] {'tensor_0'}, dimensions={0}, use_global_device_ids=true | all-gather | bytes 61440 | tf_op jit(solution)/shard_map/all_gather | solution.py:38
  217.9 0.1 fusion.2
  217.9 13.1 %all-gather.15 = f32[4,3,1024]{2,1,0:T(4,128)S(1)} all-gather(f32[1,3,1024]{2,1,0:T(4,128)S(1)} %maximum_bitcast_fusion.3), channel_id=11, replica_groups=mesh['dp_0'=4,'dp_1'=2,'tensor_0'=4,'tensor_1'=4,'pipe'=2] {'tensor_1'}, dimensions={0}, use_global_device_ids=true | all-gather | bytes 61440 | tf_op jit(solution)/shard_map/all_gather | solution.py:38
  231.1 0.6 fusion.37
  231.8 1.2 broadcast_in_dim.17
  232.9 6.6 %all-to-all-start = ((f32[2,1,1]{2,1,0:T(1,128)}), f32[2,1,1]{2,1,0:T(1,128)S(1)}, u32[]{:S(2)}, u32[]{:S(2)}) async-start(f32[2,1,1]{2,1,0:T(1,128)} %broadcast_in_dim.17), calls=%async_computation | async-start | bytes 2048 | tf_op jit(solution)/shard_map/all_to_all | solution.py:58
  239.6 0.6 dynamic-slice_bitcast_fusion
  240.2 7.1 %all-to-all-done = f32[2,1,1]{2,1,0:T(1,128)S(1)} async-done(((f32[2,1,1]{2,1,0:T(1,128)}), f32[2,1,1]{2,1,0:T(1,128)S(1)}, u32[]{:S(2)}, u32[]{:S(2)}) %all-to-all-start) | async-done | bytes 40 | tf_op jit(solution)/shard_map/all_to_all | solution.py:58
  247.3 0.6 reduce_sum.39
  (11 shorter events, 0.2 us)
Async XLA Ops:
  7.2 48.8 %all-gather.20.cloned.1.call-start = ((), (), s32[]{:S(2)}) async-start(), calls=%async_computation.1 | async-start | bytes 2293760 | tf_op jit(solution)/shard_map/all_gather | solution.py:19
  25.3 110.5 %all-gather.22.cloned.1.call-start = ((), (), s32[]{:S(2)}) async-start(), calls=%async_computation.2 | async-start | bytes 9175040 | tf_op jit(solution)/shard_map/all_gather | solution.py:19
  56.0 116.2 %all-gather.24.cloned.1.call-start = ((), (), s32[]{:S(2)}) async-start(), calls=%async_computation.3 | async-start | bytes 22020096 | tf_op jit(solution)/shard_map/all_gather | solution.py:19
  135.8 0.7 copy-start
  232.9 14.3 %all-to-all-start = ((f32[2,1,1]{2,1,0:T(1,128)}), f32[2,1,1]{2,1,0:T(1,128)S(1)}, u32[]{:S(2)}, u32[]{:S(2)}) async-start(f32[2,1,1]{2,1,0:T(1,128)} %broadcast_in_dim.17), calls=%async_computation | async-start | bytes 2048 | tf_op jit(solution)/shard_map/all_to_all | solution.py:58
Sparse Core Ops, SparseCore 0:
  25.4 30.5 all-gather.19
  57.8 77.9 all-gather.21
  137.6 33.1 all-gather.23
where the time goes:
time: 257 us; the launch traced here: 256 us
  waiting for transfers between devices  118 us (46%)
  blocking collectives  91.8 us (36%)
  between operations  15.6 us (6%)
  matrix products  12.3 us (5%)
  local copies, waits for them, and re-layouts  9.97 us (4%)
  starting transfers between devices  6.76 us (3%)
    all_gather x3, waiting for transfers between devices, gather_in_order(): pieces = lax.all_gather(pieces, axes[k])  110 us
    all_gather x5, blocking collectives, gather_in_order(): pieces = lax.all_gather(pieces, axes[k])  53.7 us
    all_gather x4, blocking collectives, all_in_one(): both, at, found = (lax.all_gather(jnp.concatenate(lines), axis), 0, {})  38.1 us
    dot_general x1, matrix products, body(): lax.dot_general(gathered, head_table, (((1,), (1,)), ((), ())), preferred...  12.3 us
    all_gather x1, local copies, waits for them, and re-layouts, gather_in_order(): pieces = lax.all_gather(pieces, axes[k])  7.45 us
    all_to_all x1, waiting for transfers between devices, copy_for_each(): lax.all_to_all(jnp.broadcast_to(value[None], (devices, *value.shape)), ax...  7.1 us
    all_to_all x1, starting transfers between devices, copy_for_each(): lax.all_to_all(jnp.broadcast_to(value[None], (devices, *value.shape)), ax...  6.64 us
  transfers between devices with their start and end apart: 4, of which 3 were waited for; matrix products, arithmetic and copies ran while one was open for 0% of the time, Pallas kernels for 0%

commit v1 on v0

v1 whole, which is shorter than its diff:
```python
import functools

import jax
import jax.numpy as jnp
from jax import lax
from jax.experimental import pallas as pl
from jax.experimental.pallas import tpu as pltpu
from jax.sharding import Mesh
from jax.sharding import PartitionSpec as P

MESH = pl.DeviceIdType.MESH
NX, NY, NZ = 4, 4, 8
TILE = 128
OWN_TOKENS = 8
ORDERS = ("xyz", "yzx", "zxy")
SLOT_OFFSET = (0, -1, 1, -2)
TABLE_CHUNKS = 10


def kernel(
    hidden, table, targets, loss_out, mean_out,
    tok, tab, acc, stat, stat_in, part, part_in,
    local_sem, table_send, table_recv, send_sem, recv_sem,
    stat_send, stat_recv, part_send, part_recv,
):
    depth = hidden.shape[2]
    rows = table.shape[0]
    width = tok.shape[4] // 3
    x, core, y = lax.axis_index("x"), lax.axis_index("core"), lax.axis_index("y")
    z_lo, pipe = lax.axis_index("z_lo"), lax.axis_index("pipe")
    z = pipe * 4 + z_lo
    sign = 1 - 2 * core
    me = {"x": x, "y": y, "z": z}
    size = {"x": NX, "y": NY, "z": NZ}

    def device(xx, cc, yy, zz):
        return (xx, cc, yy, lax.rem(zz, 4), lax.div(zz, 4))

    def moved(dim, steps):
        at = dict(me)
        at[dim] = lax.rem(me[dim] + steps * sign + size[dim], size[dim])
        return device(at["x"], core, at["y"], at["z"])

    sibling = device(x, 1 - core, y, z)

    own_hidden = pltpu.make_async_copy(
        hidden.at[0], tok.at[0, y, x, :, pl.ds(0, depth)], local_sem.at[0]
    )
    own_hidden.start()
    own_table = pltpu.make_async_copy(
        table, tab.at[core, :, pl.ds(0, depth)], local_sem.at[1]
    )
    own_table.start()

    eye = lax.broadcasted_iota(jnp.int32, (8, 8), 0) == lax.broadcasted_iota(jnp.int32, (8, 8), 1)
    ids = jnp.broadcast_to(targets[...].astype(jnp.float32), (8, 8))
    column = jnp.sum(jnp.where(eye, ids, 0.0), axis=1, keepdims=True).astype(jnp.int32)
    column = jnp.broadcast_to(column, (8, TILE))
    lane = lax.broadcasted_iota(jnp.int32, (8, TILE), 1)
    digits = jnp.where(
        lane == 0, column & 63,
        jnp.where(lane == 1, (column >> 6) & 63, jnp.where(lane == 2, column >> 12, 0)),
    )
    tok[0, y, x, :, pl.ds(depth, TILE)] = digits.astype(jnp.float32).astype(jnp.bfloat16)
    tab[:, :, pl.ds(depth, TILE)] = jnp.zeros((2, rows, TILE), jnp.bfloat16)

    barrier = pltpu.get_barrier_semaphore()
    for dim in "xyz":
        for steps in (1, -1):
            pl.semaphore_signal(barrier, inc=1, device_id=moved(dim, steps), device_id_type=MESH)
    pl.semaphore_signal(barrier, inc=1, device_id=sibling, device_id_type=MESH)
    pl.semaphore_wait(barrier, 7)
    own_hidden.wait()

    def slot_at(dim, slot):
        if dim == "z":
            return slot
        return lax.rem(me[dim] + SLOT_OFFSET[slot] * sign + 4, 4)

    def index(q, where):
        picks = [where[dim] for dim in "zyx"]
        return (*picks, slice(None), pl.ds(q * width, width))

    copies = {}
    counts = [0, 0, 0]

    def send(q, phase, kind, tag, where):
        dim = ORDERS[q][phase]
        before = 1 if kind == "R" else 0
        after = {"M": 1, "m": 2, "R": 3}[kind]
        source, target = dict(where), dict(where)
        source[dim] = slot_at(dim, before)
        target[dim] = slot_at(dim, after) if dim == "z" else source[dim]
        number = counts[q]
        counts[q] += 1
        copy = pltpu.make_async_remote_copy(
            src_ref=tok.at[index(q, source)],
            dst_ref=tok.at[index(q, target)],
            send_sem=send_sem.at[q, number],
            recv_sem=recv_sem.at[q, number],
            device_id=moved(dim, -1 if kind == "m" else 1),
            device_id_type=MESH,
        )
        copy.start()
        copies[q, phase, kind, tag] = copy

    def arrived(q, phase, kind, tag):
        copies[q, phase, kind, tag].wait_recv()

    chunk = rows // TABLE_CHUNKS
    table_copies = []

    def send_table():
        k = len(table_copies)
        if k == TABLE_CHUNKS:
            return
        copy = pltpu.make_async_remote_copy(
            src_ref=table.at[pl.ds(k * chunk, chunk), :],
            dst_ref=tab.at[core, pl.ds(k * chunk, chunk), pl.ds(0, depth)],
            send_sem=table_send.at[k],
            recv_sem=table_recv.at[k],
            device_id=sibling,
            device_id_type=MESH,
        )
        copy.start()
        table_copies.append(copy)

    def where_of(q, **slots):
        found = {}
        for name, dim in zip(("d1", "d2", "d3"), ORDERS[q]):
            slot = slots.get(name, 0)
            if slot is None:
                found[dim] = pl.ds(0, 4)
            elif isinstance(slot, tuple):
                found[dim] = pl.ds(*slot)
            else:
                found[dim] = slot_at(dim, slot)
        return found

    thirds = range(3)

    def phase1(q, kind):
        send(q, 0, kind, 0, where_of(q))

    def phase2(q, kind, j):
        send(q, 1, kind, j, where_of(q, d1=j))

    def phase3(q, kind, j):
        send(q, 2, kind, j, where_of(q, d1=None, d2=j))

    for q in thirds:
        phase1(q, "M")
        phase1(q, "m")
    for q in thirds:
        phase2(q, "M", 0)
        phase2(q, "m", 0)
    send_table()
    for q in thirds:
        arrived(q, 0, "M", 0)
        phase1(q, "R")
        phase2(q, "M", 1)
        phase2(q, "m", 1)
    for q in thirds:
        arrived(q, 0, "m", 0)
        phase2(q, "M", 2)
        phase2(q, "m", 2)
    send_table()
    for q in thirds:
        arrived(q, 1, "M", 0)
        phase2(q, "R", 0)
    for q in thirds:
        arrived(q, 0, "R", 0)
        phase2(q, "M", 3)
        phase2(q, "m", 3)
        phase3(q, "M", 0)
        phase3(q, "m", 0)
    send_table()
    for j in (1, 2):
        for q in thirds:
            arrived(q, 1, "M", j)
            phase2(q, "R", j)
        send_table()
    for q in thirds:
        arrived(q, 1, "M", 3)
        phase2(q, "R", 3)
        phase3(q, "M", 1)
        phase3(q, "m", 1)
    send_table()
    for q in thirds:
        for j in range(4):
            arrived(q, 1, "m", j)
        phase3(q, "M", 2)
        phase3(q, "m", 2)
    send_table()
    for q in thirds:
        arrived(q, 2, "M", 0)
        if q == 2:
            send(q, 2, "R", (0, 0), where_of(q, d1=(0, 2), d2=0))
        else:
            phase3(q, "R", 0)
    send_table()
    for q in thirds:
        for j in range(4):
            arrived(q, 1, "R", j)
        phase3(q, "M", 3)
        phase3(q, "m", 3)
    send_table()
    send_table()
    for j in (1, 2, 3):
        for q in thirds:
            arrived(q, 2, "M", j)
            if q == 2:
                send(q, 2, "R", (0, j), where_of(q, d1=(0, 2), d2=j))
            else:
                phase3(q, "R", j)
    for j in range(4):
        send(2, 2, "R", (1, j), where_of(2, d1=(2, 2), d2=j))
    for q in thirds:
        for j in range(4):
            arrived(q, 2, "m", j)
    own_table.wait()
    for copy in table_copies:
        copy.wait_recv()

    group = 2 * NX * NY * OWN_TOKENS

    def product(half, q):
        tokens = tok[pl.ds(2 * half, 2), :, :, :, pl.ds(q * width, width)].reshape(group, width)
        rows_of = tab[:, :, pl.ds(q * width, width)].reshape(2 * rows, width)
        return lax.dot_general(
            rows_of, tokens, (((1,), (1,)), ((), ())), preferred_element_type=jnp.float32
        )

    base = lax.rem(x * 0 + ((x * 2) * 4 + y) * 4 + z_lo, 4 * 2 * 4 * 4) * rows
    step_to_sibling = 16 * rows

    def statistics(half):
        logits = acc[...]
        top = jnp.max(logits, axis=0, keepdims=True)
        total = jnp.sum(jnp.exp(logits - top), axis=0, keepdims=True)
        coded = tok[pl.ds(2 * half, 2), :, :, :, pl.ds(depth, TILE)].reshape(group, TILE)
        place = lax.broadcasted_iota(jnp.int32, (8, TILE), 1)
        weights = jnp.where(
            place == 0, 1.0, jnp.where(place == 1, 64.0, jnp.where(place == 2, 4096.0, 0.0))
        ).astype(jnp.bfloat16)
        wanted = lax.dot_general(
            weights, coded, (((1,), (1,)), ((), ())), preferred_element_type=jnp.float32
        )[0:1].astype(jnp.int32)
        row = lax.broadcasted_iota(jnp.int32, (2 * rows, group), 0)
        entry = base + row + jnp.where(row >= rows, step_to_sibling - rows, 0)
        picked = jnp.sum(jnp.where(entry == wanted, logits, 0.0), axis=0, keepdims=True)
        spread = top + jnp.log(total)
        for k in range(2):
            lanes = slice(k * TILE, (k + 1) * TILE)
            stat[2 * half + k, 0:1, :] = spread[:, lanes]
            stat[2 * half + k, 1:2, :] = picked[:, lanes]

    mine = x * 4 + y

    def send_statistics(slot):
        owner_z = lax.rem(z + SLOT_OFFSET[slot] * sign + NZ, NZ)

        def one(k, carry):
            peer = lax.rem(mine + k, 16)
            pltpu.make_async_remote_copy(
                src_ref=stat.at[slot],
                dst_ref=stat_in.at[slot, mine],
                send_sem=stat_send.at[slot],
                recv_sem=stat_recv.at[slot],
                device_id=device(lax.div(peer, 4), core, lax.rem(peer, 4), owner_z),
                device_id_type=MESH,
            ).start()
            return carry

        lax.fori_loop(1 if slot == 0 else 0, 16, one, 0)
        if slot == 0:
            stat_in[0, mine] = stat[0]

    def wait_bytes(ref, semaphore):
        pltpu.make_async_copy(ref, ref, semaphore).wait()

    acc[...] = product(0, 0)
    arrived(1, 2, "R", 0)
    arrived(1, 2, "R", 1)
    acc[...] += product(0, 1)
    for j in range(4):
        arrived(2, 2, "R", (0, j))
    acc[...] += product(0, 2)
    statistics(0)
    send_statistics(0)
    send_statistics(1)
    for j in range(4):
        arrived(0, 2, "R", j)
    acc[...] = product(1, 0)
    arrived(1, 2, "R", 2)
    arrived(1, 2, "R", 3)
    acc[...] += product(1, 1)
    for j in range(4):
        arrived(2, 2, "R", (1, j))
    acc[...] += product(1, 2)
    statistics(1)
    send_statistics(2)
    send_statistics(3)

    for copy in copies.values():
        copy.wait_send()
    for copy in table_copies:
        copy.wait_send()
    for slot in range(4):
        count = pl.ds(0, 15 if slot == 0 else 16)
        wait_bytes(stat_in.at[slot, count], stat_send.at[slot])
        wait_bytes(stat_in.at[slot, count], stat_recv.at[slot])

    everyone = stat_in[...].reshape(64, 2, TILE)
    spreads, found = everyone[:, 0, :], everyone[:, 1, :]
    top = jnp.max(spreads, axis=0, keepdims=True)
    total = jnp.sum(jnp.exp(spreads - top), axis=0, keepdims=True)
    losses = top + jnp.log(total) - jnp.sum(found, axis=0, keepdims=True)
    part_sum = jnp.sum(losses, axis=1, keepdims=True)
    own = z * 2 + core
    part[...] = jnp.broadcast_to(part_sum, (1, TILE))
    part_in[own] = jnp.broadcast_to(part_sum, (1, TILE))

    first = (y * NX + x) * OWN_TOKENS
    shifted = pltpu.roll(jnp.broadcast_to(losses, (8, TILE)), lax.rem(TILE - first, TILE), 1)
    loss_out[...] = shifted[0:1, 0:OWN_TOKENS]

    def send_part(k, carry):
        peer = lax.rem(own + k, 2 * NZ)
        pltpu.make_async_remote_copy(
            src_ref=part,
            dst_ref=part_in.at[own],
            send_sem=part_send,
            recv_sem=part_recv,
            device_id=device(x, lax.rem(peer, 2), y, lax.div(peer, 2)),
            device_id_type=MESH,
        ).start()
        return carry

    lax.fori_loop(1, 2 * NZ, send_part, 0)
    wait_bytes(part_in.at[pl.ds(0, 2 * NZ - 1)], part_send)
    wait_bytes(part_in.at[pl.ds(0, 2 * NZ - 1)], part_recv)
    sums = jnp.sum(part_in[...].reshape(2 * NZ, TILE), axis=0, keepdims=True)
    mean_out[...] = sums[:, 0:1] / (2 * NZ * TILE)


def body(hidden, head_table, targets):
    depth, rows = hidden.shape[2], head_table.shape[0]
    dma = pltpu.SemaphoreType.DMA
    losses, mean = pl.pallas_call(
        kernel,
        out_shape=(
            jax.ShapeDtypeStruct((1, OWN_TOKENS), jnp.float32),
            jax.ShapeDtypeStruct((1, 1), jnp.float32),
        ),
        in_specs=[
            pl.BlockSpec(memory_space=pl.ANY),
            pl.BlockSpec(memory_space=pl.ANY),
            pl.BlockSpec(memory_space=pltpu.VMEM),
        ],
        out_specs=(
            pl.BlockSpec(memory_space=pltpu.VMEM),
            pl.BlockSpec(memory_space=pltpu.VMEM),
        ),
        scratch_shapes=[
            pltpu.VMEM((4, NY, NX, OWN_TOKENS, depth + TILE), jnp.bfloat16),
            pltpu.VMEM((2, rows, depth + TILE), jnp.bfloat16),
            pltpu.VMEM((2 * rows, 2 * NX * NY * OWN_TOKENS), jnp.float32),
            pltpu.VMEM((4, 2, TILE), jnp.float32),
            pltpu.VMEM((4, 16, 2, TILE), jnp.float32),
            pltpu.VMEM((1, TILE), jnp.float32),
            pltpu.VMEM((2 * NZ, 1, TILE), jnp.float32),
            dma((2,)),
            dma((TABLE_CHUNKS,)),
            dma((TABLE_CHUNKS,)),
            dma((3, 32)),
            dma((3, 32)),
            dma((4,)),
            dma((4,)),
            dma,
            dma,
        ],
        compiler_params=pltpu.CompilerParams(collective_id=0, has_side_effects=True),
        name="head_loss",
    )(hidden, head_table, targets)
    return losses, mean.reshape(())


def solution(mesh):
    split = Mesh(
        mesh.devices.reshape(NX, 2, NY, 4, 2),
        ("x", "core", "y", "z_lo", "pipe"),
    )
    shards = ("x", "core", "y", "z_lo")
    return jax.shard_map(
        body,
        mesh=split,
        in_specs=(P("pipe", shards, None), P(shards, None), P("pipe", shards)),
        out_specs=(P("pipe", shards), P()),
        check_vma=False,
    )
```

time: 257 us -> 76 us (0.30)
  the two profiles are of different devices: /device:TPU:2 before, /device:TPU:1 now
where the time goes in v1:
time: 76 us; the launch traced here: 75.9 us
  Pallas kernels  72.4 us (95%)
  between operations  2.4 us (3%)
  local copies, waits for them, and re-layouts  1.11 us (1%)
    pallas_call x1, Pallas kernels, body(): pl.pallas_call(kernel, out_shape=(jax.ShapeDtypeStruct((1, OWN_TOKENS), j...  72.4 us

profile of v1, /device:TPU:1, one launch (start us, length us, event | category | flops | bytes accessed | tf_op | source)
XLA Modules:
  0.0 75.9 jit_solution(13335887749164973124)
XLA Ops:
  0.6 72.4 %head_loss.1 = (f32[1,8]{1,0:T(1,128)}, f32[1,1]{1,0:T(1,128)}) custom-call(bf16[1,8,7168]{2,1,0:T(8,128)(2,1)} %hidden.1, bf16[640,7168]{1,0:T(8,128)(2,1)} %table.1, s32[1,8]{1,0:T(1,128)} %targets.1), custom_call_target="tpu_custom_call" | custom-call | tf_op jit(solution)/shard_map/head_loss/pallas_call | solution.py:350
  73.0 1.1 %copy.7 = f32[1,8]{1,0:T(1,128)} copy(f32[1,8]{1,0:T(1,128)} %get-tuple-element.8) | data formatting | bytes 64
